TPU v7x, 32 devices: a whole 2x2x4 slice. The times are simulated.
32 devices in a mesh: groups: 2 (over x), seq: 8 (over z, y), head: 2 (over core).
Axes of the slice: x: 2, y: 2, z: 4, core: 2. Of those that a mesh axis runs over, the one named last changes fastest.
Arguments:
- queries: bfloat16 [2048, 6144], P(('groups', 'seq', 'head')), parts along dimension 0, may hold values from -600 to 600
- latents: bfloat16 [2048, 576], P(('groups', 'seq')), parts along dimension 0, may hold values from -600 to 600
- latent_gain: float32 [512], replicated, may hold values from 0.1 to 1.9
- key_up: bfloat16 [32, 128, 512], P('head'), may hold values from -0.5 to 0.5
- value_up: bfloat16 [32, 512, 128], P('head'), may hold values from -1 to 1
- out_weight: bfloat16 [4096, 7168], P('head', 'seq'), may hold values from -0.09375 to 0.09375
Outputs:
- mixed: bfloat16 [16, 2, 64, 7168], P('groups', 'head', None, 'seq'), parts along dimension 0
There are 2 independent parts, one for each index of `groups`. A program takes and returns all parts, laid end to end along the dimension named above; an argument that names none is the same for every part. Nothing has to cross between parts.
All inputs are finite; a program needn't handle non-finite values.
Results may differ from a plain program's by a relative error of at most 0.013.
Values may be sent and summed in bfloat16 or wider, within the bound.
A program may use at most 128 MiB of HBM per device.

v0:
```python
import jax
import jax.numpy as jnp
from jax import lax
from jax.sharding import PartitionSpec as P

KV = 512
ROPE = 64
NOPE = 128
VD = 128


EPS = 1e-06


def rotate(values, position):
    middle = values.shape[-1] // 2
    frequency = 10000.0 ** (-jnp.arange(middle, dtype=jnp.float32) / middle)
    angles = position[..., None] * frequency
    former = values[..., :middle]
    latter = values[..., middle:]
    cosine = jnp.cos(angles)
    sin_part = jnp.sin(angles)
    return jnp.concatenate(
        [former * cosine - latter * sin_part, former * sin_part + latter * cosine], -1
    )


def attend(row_block, positions, key_rows, key_used, value_used):
    head_total = key_used.shape[0]
    row_total = row_block.shape[0]
    row_groups = 4
    group_rows = row_total // row_groups
    query = row_block.reshape(row_total, head_total, NOPE + ROPE)
    latent_query = jnp.einsum(
        "rhd,hdc->rhc", query[..., :NOPE], key_used, preferred_element_type=jnp.float32
    ).astype(jnp.bfloat16)
    rope_query = rotate(
        query[..., NOPE:].astype(jnp.float32), positions.astype(jnp.float32)[:, None]
    ).astype(jnp.bfloat16)
    query_rows = jnp.concatenate([latent_query, rope_query], -1).reshape(
        row_groups, group_rows, head_total, KV + ROPE
    )
    group_pos = positions.reshape(row_groups, group_rows)
    group_last = jnp.max(group_pos, axis=1)
    scale = (NOPE + ROPE) ** (-0.5)
    piece = lax.all_gather(key_rows, "seq", axis=0, tiled=True)
    start = jnp.int32(0)
    key_index = jnp.arange(piece.shape[0])
    maxima = jnp.full((row_groups, group_rows, head_total), -1e30, jnp.float32)
    totals = jnp.zeros((row_groups, group_rows, head_total), jnp.float32)
    sums = jnp.zeros((row_groups, group_rows, head_total, KV), jnp.float32)
    new_max = []
    new_tot = []
    new_sum = []
    for block in range(row_groups):

        def update(state, block=block):
            best, total, accum = state
            scores = (
                jnp.einsum(
                    "rhc,pc->rhp", query_rows[block], piece, preferred_element_type=jnp.float32
                )
                * scale
            )
            visible = key_index[None, None, :] <= group_pos[block][:, None, None]
            peak = jnp.maximum(best, jnp.max(jnp.where(visible, scores, -1e30), axis=-1))
            weights = jnp.where(visible, jnp.exp(scores - peak[..., None]), 0.0).astype(
                jnp.bfloat16
            )
            total = jnp.sum(weights.astype(jnp.float32), axis=-1)
            accum = jnp.einsum(
                "rhp,pc->rhc", weights, piece[:, :KV], preferred_element_type=jnp.float32
            )
            return (peak, total, accum)

        state = (maxima[block], totals[block], sums[block])
        state = lax.cond(start <= group_last[block], update, lambda kept: kept, state)
        new_max.append(state[0])
        new_tot.append(state[1])
        new_sum.append(state[2])
    totals = jnp.stack(new_tot)
    sums = jnp.stack(new_sum)
    latent_out = (sums / totals[..., None]).astype(jnp.bfloat16).reshape(row_total, head_total, KV)
    heads_out = jnp.einsum(
        "rhc,hcv->rhv", latent_out, value_used, preferred_element_type=jnp.float32
    )
    return heads_out.astype(jnp.bfloat16).reshape(row_total, head_total * VD)


def project(heads_out, weight):
    return jnp.dot(
        lax.all_gather(heads_out, "seq", axis=0, tiled=True),
        weight,
        preferred_element_type=jnp.float32,
    )


def local(queries, latents, latent_gain, key_up, value_up, out_weight):
    seq_index = lax.axis_index("seq")
    seq_count = lax.axis_size("seq")
    head_count = lax.axis_size("head")
    tok_block = latents.shape[0]
    latent_f = latents.astype(jnp.float32)
    compressed = latent_f[:, :KV]
    spread = jnp.mean(compressed * compressed, axis=-1, keepdims=True)
    normed = compressed * lax.rsqrt(spread + EPS) * latent_gain
    key_pos = (seq_index * tok_block + jnp.arange(tok_block)).astype(jnp.float32)
    key_rope = rotate(latent_f[:, KV:], key_pos)
    key_rows = jnp.concatenate([normed, key_rope], -1).astype(jnp.bfloat16)
    own_rows = lax.all_to_all(queries, "head", split_axis=1, concat_axis=0, tiled=True)
    key_used, value_used, proj_used = (key_up, value_up, out_weight)
    row_total = own_rows.shape[0]
    positions = seq_index * tok_block + jnp.arange(row_total)
    heads_out = attend(own_rows, positions, key_rows, key_used, value_used)
    partial_value = project(heads_out, proj_used)
    grouped = partial_value.reshape(seq_count, head_count, -1, partial_value.shape[-1])
    mixed = lax.psum_scatter(grouped.astype(jnp.bfloat16), "head", scatter_dimension=1, tiled=True)
    return mixed


def solution(mesh):
    placed = (
        P(("groups", "seq", "head"), None),
        P(("groups", "seq"), None),
        P(),
        P("head", None, None),
        P("head", None, None),
        P("head", "seq"),
    )
    return jax.shard_map(
        local,
        mesh=mesh,
        in_specs=placed,
        out_specs=P("groups", "head", None, "seq"),
        check_vma=False,
    )
```

profile of v0, /device:TPU:0, one launch (start us, length us, event | category | flops | bytes accessed | tf_op | source)
XLA Modules:
  0.0 210.7 jit_solution(8794981115084308591)
XLA Ops:
  6.6 1.1 convert_element_type.96
  7.7 0.1 multiply_reduce_fusion
  7.8 0.1 subtract_convert_fusion.1
  7.9 0.8 multiply_convert_fusion
  8.7 0.7 pad_maximum_fusion.2
  9.6 5.1 %all_to_all.16 = bf16[64,2,3072]{2,0,1:T(8,128)(2,1)} all-to-all(bf16[64,2,3072]{2,0,1:T(8,128)(2,1)S(1)} %bitcast.103), channel_id=1, replica_groups=mesh['groups'=2,'seq'=8,'head'=2] {'head'}, dimensions={1} | all-to-all | bytes 1572864 | tf_op jit(solution)/shard_map/all_to_all | solution.py:110
  14.7 2.2 %reshape.263 = bf16[128,16,192]{2,1,0:T(8,128)(2,1)S(1)} reshape(bf16[2,64,3072]{2,1,0:T(8,128)(2,1)} %bitcast.102) | data formatting | bytes 1572864 | tf_op jit(solution)/shard_map/reshape | solution.py:33
  16.9 0.9 slice.88
  17.8 0.9 slice.87
  18.7 1.5 copy.73
  20.4 0.8 convert_bitcast_fusion
  21.2 1.6 pad_maximum_fusion.1
  22.8 4.9 %copy.60 = bf16[128,16,576]{2,1,0:T(8,128)(2,1)} copy(bf16[128,16,576]{0,2,1:T(8,128)(2,1)} %pad_maximum_fusion.1) | data formatting | bytes 4718592 | tf_op jit(solution)/shard_map/concatenate | solution.py:40
  27.7 0.1 fusion.31
  27.8 0.6 fusion.32
  31.0 21.6 %all-gather.3.cloned.1.call-done = bf16[1024,576]{0,1:T(8,128)(2,1)} async-done(((bf16[128,576]{0,1:T(8,128)(2,1)}), bf16[1024,576]{0,1:T(8,128)(2,1)}) %all-gather.3.cloned.1.call-update) | async-done | bytes 1179664 | tf_op jit(solution)/shard_map/all_gather | solution.py:46
  52.7 10.0 %conditional.4 = (f32[1,32,16]{2,1,0:T(8,128)S(1)}, f32[1,32,16,512]{3,2,1,0:T(8,128)}) conditional(s32[]{:T(128)} %bitcast.24, () %tuple.53, (s32[1024]{0:T(1024)S(1)}, s32[4,32]{1,0:T(4,128)S(1)}, bf16[4,32,16,576]{3,2,1,0:T(8,128)(2,1)}, bf16[1024,576]{0,1:T(8,128)(2,1)}) %tuple.91), branch_computations={%region_2.0_spmd, %region_3.6_spmd} | conditional | flops 1147698688 | bytes 25838024 | solution.py:77
  52.7 0.1 broadcast_compare_fusion
  52.8 4.0 %select_reduce_fusion = (f32[32,16]{1,0:T(8,128)S(1)}, f32[32,16,1024]{2,1,0:T(8,128)}) fusion(pred[32,1024]{1,0:T(8,128)(4,1)S(1)} %broadcast_compare_fusion, bf16[1024,576]{0,1:T(8,128)(2,1)} %get-tuple-element.96, bf16[4,32,16,576]{3,2,1,0:T(8,128)(2,1)} %get-tuple-element.47), kind=kOutput, calls=%fused_computation.2 | convolution fusion | flops 605552128 | bytes 3966976 | tf_op jit(solution)/shard_map/cond/branch_1_fun/rhc,pc->rhp/dot_general | solution.py:60
  56.7 1.5 copy.61
  58.2 3.8 %convolution_bitcast_fusion = f32[1,32,16,512]{3,2,1,0:T(8,128)} fusion(bf16[1024,576]{1,0:T(8,128)(2,1)} %copy.61, f32[32,16,1024]{2,1,0:T(8,128)} %get-tuple-element.110, f32[32,16]{1,0:T(8,128)S(1)} %broadcast_maximum_fusion, pred[32,1024]{1,0:T(8,128)(4,1)S(1)} %broadcast_compare_fusion), kind=kOutput, calls=%fused_computation.3 | convolution fusion | flops 538968064 | bytes 4229120 | tf_op jit(solution)/shard_map/cond/branch_1_fun/rhp,pc->rhc/dot_general | solution.py:71
  62.0 0.7 convert_reduce_fusion
  62.6 10.1 %conditional.5 = (f32[1,32,16]{2,1,0:T(8,128)S(1)}, f32[1,32,16,512]{3,2,1,0:T(8,128)}) conditional(s32[]{:T(128)} %bitcast.28, () %tuple.55, (s32[1024]{0:T(1024)S(1)}, s32[4,32]{1,0:T(4,128)S(1)}, bf16[4,32,16,576]{3,2,1,0:T(8,128)(2,1)}, bf16[1024,576]{0,1:T(8,128)(2,1)}) %tuple.92), branch_computations={%region_6.7_spmd, %region_7.10_spmd} | conditional | flops 1147698688 | bytes 25838024 | solution.py:77
  62.7 0.1 broadcast_compare_fusion.1
  62.8 4.0 %select_reduce_fusion.1 = (f32[32,16]{1,0:T(8,128)S(1)}, f32[32,16,1024]{2,1,0:T(8,128)}) fusion(pred[32,1024]{1,0:T(8,128)(4,1)S(1)} %broadcast_compare_fusion.1, bf16[1024,576]{0,1:T(8,128)(2,1)} %get-tuple-element.100, bf16[4,32,16,576]{3,2,1,0:T(8,128)(2,1)} %get-tuple-element.51), kind=kOutput, calls=%fused_computation.16 | convolution fusion | flops 605552128 | bytes 3966976 | tf_op jit(solution)/shard_map/cond/branch_1_fun/rhc,pc->rhp/dot_general | solution.py:60
  66.7 1.5 copy.62
  68.2 3.8 %convolution_bitcast_fusion.1 = f32[1,32,16,512]{3,2,1,0:T(8,128)} fusion(bf16[1024,576]{1,0:T(8,128)(2,1)} %copy.62, f32[32,16,1024]{2,1,0:T(8,128)} %get-tuple-element.112, f32[32,16]{1,0:T(8,128)S(1)} %broadcast_maximum_fusion.1, pred[32,1024]{1,0:T(8,128)(4,1)S(1)} %broadcast_compare_fusion.1), kind=kOutput, calls=%fused_computation.17 | convolution fusion | flops 538968064 | bytes 4229120 | tf_op jit(solution)/shard_map/cond/branch_1_fun/rhp,pc->rhc/dot_general | solution.py:71
  72.0 0.7 convert_reduce_fusion.1
  72.7 10.0 %conditional.6 = (f32[1,32,16]{2,1,0:T(8,128)S(1)}, f32[1,32,16,512]{3,2,1,0:T(8,128)}) conditional(s32[]{:T(128)} %bitcast.29, () %tuple.56, (s32[1024]{0:T(1024)S(1)}, s32[4,32]{1,0:T(4,128)S(1)}, bf16[4,32,16,576]{3,2,1,0:T(8,128)(2,1)}, bf16[1024,576]{0,1:T(8,128)(2,1)}) %tuple.93), branch_computations={%region_10.11_spmd, %region_11.14_spmd} | conditional | flops 1147698688 | bytes 25838024 | solution.py:77
  72.7 0.1 broadcast_compare_fusion.2
  72.8 4.0 %select_reduce_fusion.2 = (f32[32,16]{1,0:T(8,128)S(1)}, f32[32,16,1024]{2,1,0:T(8,128)}) fusion(pred[32,1024]{1,0:T(8,128)(4,1)S(1)} %broadcast_compare_fusion.2, bf16[1024,576]{0,1:T(8,128)(2,1)} %get-tuple-element.104, bf16[4,32,16,576]{3,2,1,0:T(8,128)(2,1)} %get-tuple-element.55), kind=kOutput, calls=%fused_computation.30 | convolution fusion | flops 605552128 | bytes 3966976 | tf_op jit(solution)/shard_map/cond/branch_1_fun/rhc,pc->rhp/dot_general | solution.py:60
  76.8 1.5 copy.63
  78.3 3.7 %convolution_bitcast_fusion.2 = f32[1,32,16,512]{3,2,1,0:T(8,128)} fusion(bf16[1024,576]{1,0:T(8,128)(2,1)} %copy.63, f32[32,16,1024]{2,1,0:T(8,128)} %get-tuple-element.114, f32[32,16]{1,0:T(8,128)S(1)} %broadcast_maximum_fusion.2, pred[32,1024]{1,0:T(8,128)(4,1)S(1)} %broadcast_compare_fusion.2), kind=kOutput, calls=%fused_computation.31 | convolution fusion | flops 538968064 | bytes 4229120 | tf_op jit(solution)/shard_map/cond/branch_1_fun/rhp,pc->rhc/dot_general | solution.py:71
  82.0 0.7 convert_reduce_fusion.2
  82.7 10.2 %conditional.7 = (f32[1,32,16]{2,1,0:T(8,128)S(1)}, f32[1,32,16,512]{3,2,1,0:T(8,128)}) conditional(s32[]{:T(128)} %bitcast.30, () %tuple.57, (s32[1024]{0:T(1024)S(1)}, s32[4,32]{1,0:T(4,128)S(1)}, bf16[4,32,16,576]{3,2,1,0:T(8,128)(2,1)}, bf16[1024,576]{0,1:T(8,128)(2,1)}) %tuple.94), branch_computations={%region_14.15_spmd, %region_15.18_spmd} | conditional | flops 1147698688 | bytes 25838024 | solution.py:77
  82.9 0.1 broadcast_compare_fusion.3
  83.0 4.0 %select_reduce_fusion.3 = (f32[32,16]{1,0:T(8,128)S(1)}, f32[32,16,1024]{2,1,0:T(8,128)}) fusion(pred[32,1024]{1,0:T(8,128)(4,1)S(1)} %broadcast_compare_fusion.3, bf16[1024,576]{0,1:T(8,128)(2,1)} %get-tuple-element.108, bf16[4,32,16,576]{3,2,1,0:T(8,128)(2,1)} %get-tuple-element.59), kind=kOutput, calls=%fused_computation.44 | convolution fusion | flops 605552128 | bytes 3966976 | tf_op jit(solution)/shard_map/cond/branch_1_fun/rhc,pc->rhp/dot_general | solution.py:60
  87.0 1.5 copy.64
  88.4 3.7 %convolution_bitcast_fusion.3 = f32[1,32,16,512]{3,2,1,0:T(8,128)} fusion(bf16[1024,576]{1,0:T(8,128)(2,1)} %copy.64, f32[32,16,1024]{2,1,0:T(8,128)} %get-tuple-element.116, f32[32,16]{1,0:T(8,128)S(1)} %broadcast_maximum_fusion.3, pred[32,1024]{1,0:T(8,128)(4,1)S(1)} %broadcast_compare_fusion.3), kind=kOutput, calls=%fused_computation.45 | convolution fusion | flops 538968064 | bytes 4229120 | tf_op jit(solution)/shard_map/cond/branch_1_fun/rhp,pc->rhc/dot_general | solution.py:71
  92.2 0.7 convert_reduce_fusion.3
  92.9 2.8 %pad_maximum_fusion = f32[4,32,16,512]{3,2,1,0:T(8,128)S(1)} fusion(f32[1,32,16,512]{3,2,1,0:T(8,128)} %get-tuple-element.72, f32[1,32,16,512]{3,2,1,0:T(8,128)} %get-tuple-element.71, f32[1,32,16,512]{3,2,1,0:T(8,128)} %get-tuple-element.70, f32[1,32,16,512]{3,2,1,0:T(8,128)} %get-tuple-element.69), kind=kLoop, calls=%fused_computation.56 | loop fusion | flops 3145728 | bytes 8388608 | tf_op jit(solution)/shard_map/stack | solution.py:82
  95.7 0.1 copy-done.11
  95.8 3.7 %fusion.27 = bf16[16,128,128]{1,2,0:T(8,128)(2,1)} fusion(bf16[16,512,128]{2,1,0:T(8,128)(2,1)S(1)} %copy-done.11, f32[128,16,512]{2,1,0:T(8,128)S(1)} %bitcast.101, f32[128,16]{0,1:T(8,128)S(1)} %copy.65), kind=kOutput, calls=%fused_computation.63 | convolution fusion | flops 270794752 | bytes 6823936 | tf_op jit(solution)/shard_map/rhc,hcv->rhv/dot_general | solution.py:84
  99.6 73.5 %all-gather.5.cloned.1.call-done = bf16[1024,2048]{0,1:T(8,128)(2,1)} async-done(((bf16[128,2048]{0,1:T(8,128)(2,1)}), bf16[1024,2048]{0,1:T(8,128)(2,1)}) %all-gather.5.cloned.1.call-update) | async-done | bytes 4194320 | tf_op jit(solution)/shard_map/all_gather | solution.py:92
  173.1 9.2 %convolution_convert_fusion = bf16[1024,896]{1,0:T(8,128)(2,1)} fusion(bf16[1024,2048]{0,1:T(8,128)(2,1)} %all-gather.5.cloned.1.call-done, bf16[2048,896]{1,0:T(8,128)(2,1)} %param.19), kind=kOutput, calls=%fused_computation.62 | convolution fusion | flops 3759013888 | bytes 9699328 | tf_op jit(solution)/shard_map/dot_general | solution.py:91
  182.3 0.6 dynamic-slice
  182.9 18.6 %all-reduce.3.cloned.1.call-done = bf16[8,2,64,896]{3,2,1,0:T(8,128)(2,1)} async-done(((bf16[8,2,64,896]{3,2,1,0:T(8,128)(2,1)}), bf16[8,2,64,896]{3,2,1,0:T(8,128)(2,1)}) %all-reduce.3.cloned.1.call-update) | async-done | bytes 1835024
  201.5 2.7 %constant_dynamic-slice_fusion = bf16[8,1,64,896]{3,2,1,0:T(8,128)(2,1)} fusion(bf16[8,2,64,896]{3,2,1,0:T(8,128)(2,1)} %all-reduce.3.cloned.1.call-done, u32[]{:T(128)} %bitcast.43), kind=kLoop, calls=%fused_computation.78 | loop fusion | bytes 1835012
  (49 shorter events, 0.5 us)
Async XLA Ops:
  6.5 13.9 %copy-start = (bf16[16,128,512]{2,1,0:T(8,128)(2,1)S(1)}, bf16[16,128,512]{2,1,0:T(8,128)(2,1)}, u32[]{:S(2)}) copy-start(bf16[16,128,512]{2,1,0:T(8,128)(2,1)} %param.17) | copy-start | bytes 6291460
  6.5 3.0 %copy-start.10 = (bf16[64,6144]{1,0:T(8,128)(2,1)S(1)}, bf16[64,6144]{1,0:T(8,128)(2,1)}, u32[]{:S(2)}) copy-start(bf16[64,6144]{1,0:T(8,128)(2,1)} %param.14) | copy-start | bytes 2359300
  6.5 46.1 %all-gather.3.cloned.1.call-start = ((), (), s32[]{:S(2)}) async-start(), calls=%async_computation.1 | async-start | bytes 1327104 | tf_op jit(solution)/shard_map/all_gather | solution.py:46
  9.4 163.7 %all-gather.5.cloned.1.call-start = ((), (), s32[]{:S(2)}) async-start(), calls=%async_computation.2 | async-start | bytes 4718592 | tf_op jit(solution)/shard_map/all_gather | solution.py:92
  18.7 1.7 copy-start.5
  52.8 4.0 %copy-start.1 = (bf16[1024,576]{0,1:T(8,128)(2,1)S(1)}, bf16[1024,576]{0,1:T(8,128)(2,1)}, u32[]{:S(2)}) copy-start(bf16[1024,576]{0,1:T(8,128)(2,1)} %get-tuple-element.96) | copy-start | bytes 3538948 | tf_op jit(solution)/shard_map/cond
  58.2 3.8 %copy-start.6 = (f32[32,16,1024]{2,1,0:T(8,128)S(1)}, f32[32,16,1024]{2,1,0:T(8,128)}, u32[]{:S(2)}) copy-start(f32[32,16,1024]{2,1,0:T(8,128)} %get-tuple-element.110) | copy-start | bytes 6291460 | tf_op jit(solution)/shard_map/cond
  62.8 4.0 %copy-start.2 = (bf16[1024,576]{0,1:T(8,128)(2,1)S(1)}, bf16[1024,576]{0,1:T(8,128)(2,1)}, u32[]{:S(2)}) copy-start(bf16[1024,576]{0,1:T(8,128)(2,1)} %get-tuple-element.100) | copy-start | bytes 3538948 | tf_op jit(solution)/shard_map/cond
  68.2 3.8 %copy-start.7 = (f32[32,16,1024]{2,1,0:T(8,128)S(1)}, f32[32,16,1024]{2,1,0:T(8,128)}, u32[]{:S(2)}) copy-start(f32[32,16,1024]{2,1,0:T(8,128)} %get-tuple-element.112) | copy-start | bytes 6291460 | tf_op jit(solution)/shard_map/cond
  72.8 4.0 %copy-start.3 = (bf16[1024,576]{0,1:T(8,128)(2,1)S(1)}, bf16[1024,576]{0,1:T(8,128)(2,1)}, u32[]{:S(2)}) copy-start(bf16[1024,576]{0,1:T(8,128)(2,1)} %get-tuple-element.104) | copy-start | bytes 3538948 | tf_op jit(solution)/shard_map/cond
  78.3 3.7 %copy-start.8 = (f32[32,16,1024]{2,1,0:T(8,128)S(1)}, f32[32,16,1024]{2,1,0:T(8,128)}, u32[]{:S(2)}) copy-start(f32[32,16,1024]{2,1,0:T(8,128)} %get-tuple-element.114) | copy-start | bytes 6291460 | tf_op jit(solution)/shard_map/cond
  83.0 4.0 %copy-start.4 = (bf16[1024,576]{0,1:T(8,128)(2,1)S(1)}, bf16[1024,576]{0,1:T(8,128)(2,1)}, u32[]{:S(2)}) copy-start(bf16[1024,576]{0,1:T(8,128)(2,1)} %get-tuple-element.108) | copy-start | bytes 3538948 | tf_op jit(solution)/shard_map/cond
  88.4 3.7 %copy-start.9 = (f32[32,16,1024]{2,1,0:T(8,128)S(1)}, f32[32,16,1024]{2,1,0:T(8,128)}, u32[]{:S(2)}) copy-start(f32[32,16,1024]{2,1,0:T(8,128)} %get-tuple-element.116) | copy-start | bytes 6291460 | tf_op jit(solution)/shard_map/cond
  92.9 2.9 %copy-start.11 = (bf16[16,512,128]{2,1,0:T(8,128)(2,1)S(1)}, bf16[16,512,128]{2,1,0:T(8,128)(2,1)}, u32[]{:S(2)}) copy-start(bf16[16,512,128]{2,1,0:T(8,128)(2,1)} %param.18) | copy-start | bytes 6291460
  99.5 82.8 %copy-start.12 = (u32[32]{0:T(128)S(1)}, u32[32]{0:T(128)}, u32[]{:S(2)}) copy-start(u32[32]{0:T(128)} %constant.80) | copy-start | bytes 388
  99.5 101.9 %all-reduce.3.cloned.1.call-start = ((), (), s32[]{:S(2)}) async-start(), calls=%async_computation.3 | async-start | bytes 3670016
Sparse Core Ops, SparseCore 0:
  9.6 43.0 all-gather.2
  99.6 73.4 all-gather.4
  182.4 19.0 all-reduce.2
where the time goes:
time: 211 us
  waiting for transfers between devices  114 us (54%)
  matrix products  44.6 us (21%)
  local copies, waits for them, and re-layouts  20.5 us (10%)
  between operations  15.8 us (7%)
  other arithmetic  10.5 us (5%)
  blocking collectives  5.14 us (2%)
    all_gather x1, waiting for transfers between devices, project(): lax.all_gather(heads_out, 'seq', axis=0, tiled=True)  73.5 us
    all_gather x1, waiting for transfers between devices, attend(): piece = lax.all_gather(key_rows, 'seq', axis=0, tiled=True)  21.6 us
    unnamed x4, waiting for transfers between devices  18.7 us
    dot_general x4, matrix products, update(): jnp.einsum('rhc,pc->rhp', query_rows[block], piece, preferred_element_typ...  15.8 us
    dot_general x4, matrix products, update(): jnp.einsum('rhp,pc->rhc', weights, piece[:, :KV], preferred_element_type=...  15.1 us
    dot_general x1, matrix products, project(): jnp.dot(lax.all_gather(heads_out, 'seq', axis=0, tiled=True), weight, pre...  9.17 us
    another operation x4, local copies, waits for them, and re-layouts  5.89 us
    all_to_all x1, blocking collectives, local(): lax.all_to_all(queries, 'head', split_axis=1, concat_axis=0, tiled=True)  5.14 us
  transfers between devices with their start and end apart: 3, of which 3 were waited for; matrix products, arithmetic and copies ran while one was open for 7% of the time, Pallas kernels for 0%

commit v1 on v0

v1 whole, which is shorter than its diff:
```python
import functools
import math

import jax
import jax.numpy as jnp
from jax import lax
from jax.experimental import pallas as pl
from jax.experimental.pallas import tpu as pltpu
from jax.sharding import PartitionSpec as P

MESH = pl.DeviceIdType.MESH
EPS = 1e-06
LANES = 128


def kernel(
    n,
    dims,
    q_hbm,
    lat_ref,
    gain_ref,
    tab_ref,
    kup_hbm,
    vup_hbm,
    w_hbm,
    out_ref,
    q_all,
    q_rows,
    keys,
    kup,
    vup,
    w,
    gath,
    part,
    own,
    sbuf,
    rbuf,
    local_sem,
    q_send,
    q_recv,
    k_send,
    k_recv,
    d_send,
    d_recv,
    r_send,
    r_recv,
    x_send,
    x_recv,
):
    heads, nope, rope, kv, vd, group = dims
    rows = lat_ref.shape[0]
    half_rows = rows // 2
    groups = heads // group
    total = n * rows
    slab = 2 * (nope + rope)
    width = keys.shape[-1]
    half_n = (n + 1) // 2
    gidx = lax.axis_index("groups")
    sidx = lax.axis_index("seq")
    h = lax.axis_index("head")
    odd = lax.rem(sidx, 2)
    place = (1 - odd) * (sidx // 2) + odd * (n - 1 - sidx // 2)

    def seq_of(position):
        position = lax.rem(position + 2 * n, n)
        upper = position // half_n
        return (1 - upper) * (2 * position) + upper * (2 * (n - 1 - position) + 1)

    partner = (gidx, sidx, 1 - h)

    half_cols = heads * (nope + rope)
    loads = [
        pltpu.make_async_copy(
            q_hbm.at[:, pl.ds(pl.multiple_of(h * half_cols, LANES), half_cols)],
            q_all.at[pl.ds(pl.multiple_of(h * half_rows, 16), half_rows)],
            local_sem.at[0],
        ),
        pltpu.make_async_copy(kup_hbm, kup, local_sem.at[1]),
        pltpu.make_async_copy(vup_hbm, vup, local_sem.at[2]),
        pltpu.make_async_copy(w_hbm, w, local_sem.at[3]),
    ]
    for load in loads:
        load.start()

    barrier = pltpu.get_barrier_semaphore()
    for other in ((gidx, seq_of(place + 1), h), (gidx, seq_of(place - 1), h), partner):
        pl.semaphore_signal(barrier, inc=1, device_id=other, device_id_type=MESH)

    latent = lat_ref[...].astype(jnp.float32)
    compressed = latent[:, :kv]
    spread = jnp.mean(compressed * compressed, axis=-1, keepdims=True)
    normed = compressed * lax.rsqrt(spread + EPS) * gain_ref[...]

    def rotate(raw):
        return (
            raw * tab_ref[0]
            + pltpu.roll(raw, LANES - rope // 2, 1) * tab_ref[1]
            + pltpu.roll(raw, rope // 2, 1) * tab_ref[2]
        )

    tail = jnp.concatenate(
        [latent[:, kv:], jnp.zeros((rows, LANES - rope), jnp.float32)], axis=1
    )
    keys[sidx, :, :kv] = normed.astype(jnp.bfloat16)
    keys[sidx, :, kv:] = rotate(tail).astype(jnp.bfloat16)

    pl.semaphore_wait(barrier, 3)

    q_copy = pltpu.make_async_remote_copy(
        src_ref=q_hbm.at[:, pl.ds(pl.multiple_of((1 - h) * half_cols, LANES), half_cols)],
        dst_ref=q_all.at[pl.ds(pl.multiple_of(h * half_rows, 16), half_rows)],
        send_sem=q_send,
        recv_sem=q_recv,
        device_id=partner,
        device_id_type=MESH,
    )

    def key_hop(way, step):
        sign = 1 - 2 * way
        piece = keys.at[
            seq_of(place - sign * step), pl.ds(pl.multiple_of(h * half_rows, 16), half_rows)
        ]
        return pltpu.make_async_remote_copy(
            src_ref=piece,
            dst_ref=piece,
            send_sem=k_send.at[way, step],
            recv_sem=k_recv.at[way, step],
            device_id=(gidx, seq_of(place + sign), h),
            device_id_type=MESH,
        )

    def key_pass(way, step, side):
        sign = 1 - 2 * way
        piece = keys.at[
            seq_of(place - sign * (step + 1)),
            pl.ds(pl.multiple_of(side * half_rows, 16), half_rows),
        ]
        return pltpu.make_async_remote_copy(
            src_ref=piece,
            dst_ref=piece,
            send_sem=d_send.at[way, step],
            recv_sem=d_recv.at[way, step],
            device_id=partner,
            device_id_type=MESH,
        )

    hops = (n // 2, n - 1 - n // 2)
    for way in range(2):
        if hops[way] > 0:
            key_hop(way, 0).start()
    q_copy.start()
    loads[0].wait()
    loads[1].wait()

    def lift(pair):
        start = pl.multiple_of(pair * slab, LANES)
        first = q_all[:, pl.ds(start, nope)]
        second = q_all[:, pl.ds(pl.multiple_of(start + nope, LANES), slab - nope)].astype(
            jnp.float32
        )
        moved = pltpu.roll(second, slab - nope - rope, 1)
        raws = (second[:, :LANES], moved[:, nope : nope + LANES])
        flat = (first, moved[:, :nope].astype(jnp.bfloat16))
        for i in range(2):
            head = 2 * pair + i
            q_rows[head, :, :kv] = jnp.dot(
                flat[i], kup[head], preferred_element_type=jnp.float32
            ).astype(jnp.bfloat16)
            q_rows[head, :, kv:] = rotate(raws[i]).astype(jnp.bfloat16)

    def key_step(step):
        for way in range(2):
            if step <= hops[way]:
                key_hop(way, step - 1).wait_recv()
                if step < hops[way]:
                    key_hop(way, step).start()
                key_pass(way, step - 1, h).start()

    pairs = heads // 2
    per_step = -(-pairs // max(hops[0], 1))
    done = 0
    q_copy.wait_recv()
    for step in range(1, hops[0] + 1):
        count = min(per_step, pairs - done)
        if count > 0:

            def some(i, carry):
                lift(i)
                return carry

            lax.fori_loop(done, done + count, some, 0)
            done += count
        key_step(step)
    for way in range(2):
        for step in range(hops[way]):
            key_pass(way, step, h).wait_recv()
    loads[2].wait()

    def ring_hop(chunk, step):
        sign = 1 - 2 * lax.rem(chunk, 2)
        piece = gath.at[seq_of(place - sign * step), chunk]
        return pltpu.make_async_remote_copy(
            src_ref=piece,
            dst_ref=piece,
            send_sem=r_send.at[chunk, step],
            recv_sem=r_recv.at[chunk, step],
            device_id=(gidx, seq_of(place + sign), h),
            device_id_type=MESH,
        )

    factor = (nope + rope) ** (-0.5) * math.log2(math.e)

    def attend(g, carry):
        query = q_rows[pl.ds(g * group, group)].reshape(group * rows, width)
        all_keys = keys[...].reshape(total, width)
        scores = lax.dot_general(
            query, all_keys, (((1,), (1,)), ((), ())), preferred_element_type=jnp.float32
        )
        column = lax.broadcasted_iota(jnp.int32, (rows, total), 1)
        line = lax.broadcasted_iota(jnp.int32, (rows, total), 0) + sidx * rows
        visible = column <= line
        scores = jnp.where(visible[None], scores.reshape(group, rows, total), -1e30)
        peak = jnp.max(scores, axis=-1, keepdims=True)
        probs = jnp.exp2((scores - peak) * factor).astype(jnp.bfloat16)
        sums = jnp.sum(probs.astype(jnp.float32), axis=-1, keepdims=True)
        mixed = jnp.dot(
            probs.reshape(group * rows, total),
            all_keys[:, :kv],
            preferred_element_type=jnp.float32,
        ).reshape(group, rows, kv)
        latent_out = (mixed / sums).astype(jnp.bfloat16)
        for i in range(group):
            gath[sidx, g, :, i * vd : (i + 1) * vd] = jnp.dot(
                latent_out[i], vup[g * group + i], preferred_element_type=jnp.float32
            ).astype(jnp.bfloat16)
        ring_hop(g, 0).start()

        @pl.when(g >= 2)
        def _():
            ring_hop(g - 2, 0).wait_recv()
            ring_hop(g - 2, 1).start()

        return carry

    lax.fori_loop(0, groups, attend, 0)
    loads[3].wait()

    def exchange(block):
        return pltpu.make_async_remote_copy(
            src_ref=sbuf.at[block],
            dst_ref=rbuf.at[block],
            send_sem=x_send.at[block],
            recv_sem=x_recv.at[block],
            device_id=partner,
            device_id_type=MESH,
        )

    def finish(block):
        value = None
        for c in range(groups):
            term = jnp.dot(gath[block, c], w[c], preferred_element_type=jnp.float32)
            value = term if value is None else value + term
        part[...] = value.reshape(part.shape)
        sbuf[block] = part[1 - h].astype(jnp.bfloat16)
        own[block] = part[h]
        exchange(block).start()

    for c in range(max(groups - 2, 0), groups):
        ring_hop(c, 0).wait_recv()
        ring_hop(c, 1).start()
    finish(sidx)

    def ring_step(step, carry):
        for c in range(groups):
            ring_hop(c, step - 1).wait_recv()

            @pl.when(step < n - 1)
            def _():
                ring_hop(c, step).start()

        @pl.when(2 * step >= n)
        def _():
            finish(seq_of(place - step))

        @pl.when(2 * step > n)
        def _():
            finish(seq_of(place + step))

        return carry

    lax.fori_loop(2, n, ring_step, 0)

    def close(step, carry):
        block = seq_of(place + step)
        exchange(block).wait_recv()
        out_ref[block] = (own[block] + rbuf[block].astype(jnp.float32)).astype(out_ref.dtype)
        exchange(block).wait_send()
        return carry

    lax.fori_loop(0, n, close, 0)

    q_copy.wait_send()
    for way in range(2):
        for step in range(hops[way]):
            key_hop(way, step).wait_send()
            key_pass(way, step, h).wait_send()

    def drain(step, carry):
        for c in range(groups):
            ring_hop(c, step).wait_send()
        return carry

    lax.fori_loop(0, n - 1, drain, 0)


def local(queries, latents, latent_gain, key_up, value_up, out_weight):
    n = lax.axis_size("seq")
    seq_index = lax.axis_index("seq")
    heads, nope, kv = key_up.shape
    vd = value_up.shape[-1]
    rope = latents.shape[-1] - kv
    rows = latents.shape[0]
    columns = out_weight.shape[-1]
    group = 4 if heads % 8 == 0 and n * rows <= 2048 else 2
    chunks = heads // group
    width = kv + LANES
    half = rope // 2
    frequency = 10000.0 ** (-jnp.arange(half, dtype=jnp.float32) / half)
    position = (seq_index * rows + jnp.arange(rows)).astype(jnp.float32)
    angles = position[:, None] * frequency
    cosine, sine = jnp.cos(angles), jnp.sin(angles)
    zero = jnp.zeros_like(sine)
    fill = jnp.zeros((rows, LANES - rope), jnp.float32)
    table = jnp.stack(
        [
            jnp.concatenate([cosine, cosine, fill], -1),
            jnp.concatenate([-sine, zero, fill], -1),
            jnp.concatenate([zero, sine, fill], -1),
        ]
    )
    bf16, f32 = jnp.bfloat16, jnp.float32
    dma = pltpu.SemaphoreType.DMA
    hops = max(n // 2, 1)
    any_spec = pl.BlockSpec(memory_space=pl.ANY)
    vmem_spec = pl.BlockSpec(memory_space=pltpu.VMEM)
    out = pl.pallas_call(
        functools.partial(kernel, n, (heads, nope, rope, kv, vd, group)),
        out_shape=jax.ShapeDtypeStruct((n, rows // 2, columns), bf16),
        in_specs=[any_spec, vmem_spec, vmem_spec, vmem_spec, any_spec, any_spec, any_spec],
        out_specs=vmem_spec,
        scratch_shapes=[
            pltpu.VMEM((rows, heads * (nope + rope)), bf16),
            pltpu.VMEM((heads, rows, width), bf16),
            pltpu.VMEM((n, rows, width), bf16),
            pltpu.VMEM(key_up.shape, bf16),
            pltpu.VMEM(value_up.shape, bf16),
            pltpu.VMEM((chunks, group * vd, columns), bf16),
            pltpu.VMEM((n, chunks, rows, group * vd), bf16),
            pltpu.VMEM((2, rows // 2, columns), f32),
            pltpu.VMEM((n, rows // 2, columns), f32),
            pltpu.VMEM((n, rows // 2, columns), bf16),
            pltpu.VMEM((n, rows // 2, columns), bf16),
            dma((4,)),
            dma,
            dma,
            dma((2, hops)),
            dma((2, hops)),
            dma((2, hops)),
            dma((2, hops)),
            dma((chunks, n - 1)),
            dma((chunks, n - 1)),
            dma((n,)),
            dma((n,)),
        ],
        compiler_params=pltpu.CompilerParams(
            collective_id=0, has_side_effects=True, vmem_limit_bytes=66 * 1000 * 1000
        ),
        name="layer",
    )(
        queries,
        latents,
        latent_gain.reshape(1, kv),
        table,
        key_up,
        value_up,
        out_weight.reshape(chunks, group * vd, columns),
    )
    return out.reshape(n, 1, rows // 2, columns)


def solution(mesh):
    placed = (
        P(("groups", "seq", "head"), None),
        P(("groups", "seq"), None),
        P(),
        P("head", None, None),
        P("head", None, None),
        P("head", "seq"),
    )
    return jax.shard_map(
        local,
        mesh=mesh,
        in_specs=placed,
        out_specs=P("groups", "head", None, "seq"),
        check_vma=False,
    )
```

time: 211 us -> 77.9 us (0.37)
  waiting for transfers between devices: 114 us -> 0 us
  Pallas kernels: 0 us -> 72.5 us
  matrix products: 44.6 us -> 0 us
  local copies, waits for them, and re-layouts: 20.5 us -> 3.97 us
  between operations: 15.8 us -> 0.03 us
  other arithmetic: 10.5 us -> 1.13 us
  blocking collectives: 5.14 us -> 0 us
    all_gather x2 -> x0, waiting for transfers between devices: 95.2 us -> none  [the longest x1 73.5 us: project(): lax.all_gather(heads_out, 'seq', axis=0, tiled=True)]
    pallas_call x0 -> x1, Pallas kernels: none -> 72.5 us  [local(): pl.pallas_call(functools.partial(kernel, n, (heads, nope, rope, kv, vd, g...]
    dot_general x11 -> x0, matrix products: 44.6 us -> none  [the longest x4 15.8 us: update(): jnp.einsum('rhc,pc->rhp', query_rows[block], piece, preferred_element_typ...]
    unnamed x4 -> x0, waiting for transfers between devices: 18.7 us -> none
    another operation x4 -> x0, local copies, waits for them, and re-layouts: 5.89 us -> none
    all_to_all x1 -> x0, blocking collectives: 5.14 us -> none  [local(): lax.all_to_all(queries, 'head', split_axis=1, concat_axis=0, tiled=True)]
    concatenate x1, local copies, waits for them, and re-layouts: 4.91 us -> 0.08 us  [local(): jnp.concatenate([cosine, cosine, fill], -1)]
    another operation x9 -> x2, other arithmetic: 3.86 us -> 0.81 us  [local(): jnp.stack([jnp.concatenate([cosine, cosine, fill], -1), jnp.concatenate([...]
  transfers between devices with their start and end apart: 3 -> 0, of which waited for: 3 -> 0; matrix products, arithmetic and copies ran while one was open for 7% -> 0% of each run, Pallas kernels for 0% -> 0%
where the time goes in v1:
time: 77.9 us; the launch traced here: 77.7 us
  Pallas kernels  72.5 us (93%)
  local copies, waits for them, and re-layouts  3.97 us (5%)
  other arithmetic  1.13 us (1%)
    pallas_call x1, Pallas kernels, local(): pl.pallas_call(functools.partial(kernel, n, (heads, nope, rope, kv, vd, g...  72.5 us
    unnamed x2, local copies, waits for them, and re-layouts  3.89 us

profile of v1, /device:TPU:0, one launch (start us, length us, event | category | flops | bytes accessed | tf_op | source)
XLA Modules:
  0.0 77.7 jit_solution(2563612948919550833)
XLA Ops:
  0.0 0.1 pad.11.clone
  0.1 1.7 %copy.7.lat_ref = bf16[128,576]{1,0:T(8,128)(2,1)} copy(bf16[128,576]{0,1:T(8,128)(2,1)} %param.7) | data formatting | bytes 294912 | tf_op args[1]
  1.8 0.3 multiply_cosine_fusion
  2.1 0.1 maximum_bitcast_fusion.1
  2.3 0.7 pad_maximum_fusion.tab_ref
  3.0 72.5 %layer.1 = bf16[8,64,896]{2,1,0:T(8,128)(2,1)} custom-call(bf16[64,6144]{1,0:T(8,128)(2,1)} %q_hbm.1, bf16[128,576]{1,0:T(8,128)(2,1)} %copy.7.lat_ref, f32[1,512]{1,0:T(1,128)} %bitcast.13, f32[3,128,128]{2,1,0:T(8,128)} %pad_maximum_fusion.tab_ref, bf16[16,128,512]{2,1,0:T(8,128)(2,1)} %kup_hbm.1, bf16[16,512,128]{2,1,0:T(8,128)(2,1)} %vup_hbm.1, ...), custom_call_target="tpu_custom_call" | custom-call | tf_op jit(solution)/shard_map/layer/pallas_call | solution.py:346
  75.5 2.2 %copy.10 = bf16[8,1,64,896]{3,2,1,0:T(8,128)(2,1)} copy(bf16[8,1,64,896]{3,2,1,0:T(8,128)(2,1)} %bitcast.12) | data formatting | bytes 1835008
  (4 shorter events, 0.0 us)
